TPU v7x, 256 devices: a whole 4x4x8 slice. The times are simulated.
256 devices in a mesh: grid: 8 (over z), orb: 16 (over y, x_hi, core), pts: 2 (over x_lo).
Axes of the slice: x: 4 (x_hi: 2, x_lo: 2; x = x_hi * 2 + x_lo), y: 4, z: 8, core: 2. Of those that a mesh axis runs over, the one named last changes fastest.
Arguments:
- orbitals: bfloat16 [2048, 2048], P('grid', 'orb'), may hold values from -6 to 6
- points: int32 [8192], replicated, may hold values from 0 to 2047
- fitting: bfloat16 [2048, 8192], P('grid', ('orb', 'pts')), may hold values from -0.0625 to 0.0625
- screened: bfloat16 [8192, 8192], P(('orb', 'pts'), 'grid'), may hold values from -0.0014648438 to 0.0014648438
Outputs:
- exchange_orbitals: float32 [2048, 2048], P(('orb', 'pts'), 'grid')
- exchange_matrix: float32 [2048, 2048], P(('orb', 'pts'), 'grid')
Inputs may be any that keep to these rules, and one draw needn't show every extreme that they name: Grid rows of the window; two points may name the same row.
All inputs are finite; a program needn't handle non-finite values.
Results may differ from a plain program's by a relative error of at most 0.005.
Values may be sent and summed in bfloat16 or wider, within the bound.
No kernel may reach another device: no remote copies, remote signals or barrier semaphores. Data moves between devices by JAX's collectives and lax.ppermute only.
A program may use at most 128 MiB of HBM per device.

v0:
```python
import math
import jax
import jax.numpy as jnp
from jax import lax
from jax.sharding import PartitionSpec as P


def in_one_piece(arrays, axis, dim, along):
    widths = [a.shape[along] for a in arrays]
    both = jnp.concatenate(arrays, axis=along)
    filled = lax.all_gather(both, axis, axis=dim, tiled=True)
    return tuple(jnp.split(filled, [sum(widths[:k]) for k in range(1, len(widths))], axis=along))


def laid_out(parts, dim):
    parts = jnp.moveaxis(parts, 0, dim)
    shape = parts.shape
    return parts.reshape(*shape[:dim], shape[dim] * shape[dim + 1], *shape[dim + 2 :])


def sent_to_all(x, axis):
    copies = jnp.broadcast_to(x, (lax.axis_size(axis), *x.shape))
    return lax.all_to_all(copies, axis, split_axis=0, concat_axis=0, tiled=True)


def collect(x, axis, dim):
    return laid_out(sent_to_all(x, axis), dim)


def split_up(x, dim, peers):
    shape = x.shape
    parts = x.reshape(*shape[:dim], peers, shape[dim] // peers, *shape[dim + 1 :])
    return jnp.moveaxis(parts, dim, 0)


def sent_and_summed(x, axis, dim):
    peers = lax.axis_size(axis)
    parts = lax.all_to_all(split_up(x, dim, peers), axis, 0, 0, tiled=True)
    return jnp.sum(parts, axis=0)


def per_device(orbitals, points, fitting, screened):
    grid_index = lax.axis_index("grid")
    orb_index = lax.axis_index("orb")
    pts_index = lax.axis_index("pts")
    n_grid = lax.axis_size("grid")
    n_orb = lax.axis_size("orb")
    n_pts = lax.axis_size("pts")
    rows_dev, width_dev = orbitals.shape
    npoints = points.shape[0]
    nfull = width_dev * n_orb
    point_block = npoints // (n_orb * n_pts)
    column_block = npoints // n_grid
    orbital_block = nfull // (n_orb * n_pts)
    local_rows = points - grid_index * rows_dev
    inside = (local_rows >= 0) & (local_rows < rows_dev)
    clamped = jnp.clip(local_rows, 0, rows_dev - 1)
    taken = jnp.take(orbitals, clamped, axis=0).astype(jnp.float32)
    selected = jnp.where(inside[:, None], taken, jnp.zeros_like(taken))
    picked = lax.psum(selected.astype(jnp.bfloat16), "grid")
    grouped = picked.reshape(n_orb, n_pts, point_block, width_dev)
    own_rows = lax.dynamic_index_in_dim(grouped, pts_index, 1, keepdims=False).reshape(
        n_orb * point_block, width_dev
    )
    point_rows = lax.dynamic_slice_in_dim(picked, grid_index * column_block, column_block, 0)
    rows_full, point_full = in_one_piece((own_rows, point_rows), "orb", 1, 0)
    own_full = lax.dynamic_slice_in_dim(rows_full, orb_index * point_block, point_block, 0)
    density = lax.dot_general(
        own_full, point_full, (((1,), (1,)), ((), ())), preferred_element_type=jnp.float32
    )
    masked = (density * screened.astype(jnp.float32)).astype(jnp.bfloat16)
    partial_applied = jnp.dot(masked, point_full, preferred_element_type=jnp.float32)
    applied = lax.psum(partial_applied, "grid").astype(jnp.bfloat16)
    columns = lax.all_to_all(applied, ("orb", "pts"), split_axis=1, concat_axis=0, tiled=True)
    initial = jnp.zeros((orbital_block, rows_dev), jnp.float32)
    terms = initial - lax.dot_general(
        columns,
        lax.all_gather(fitting, ("orb", "pts"), axis=1, tiled=True),
        (((0,), (1,)), ((), ())),
        preferred_element_type=jnp.float32,
    )
    rounded = terms.astype(jnp.bfloat16)
    partial_matrix = jnp.dot(
        rounded, collect(orbitals, "orb", 1), preferred_element_type=jnp.float32
    )
    summed = sent_and_summed(partial_matrix, "grid", 1)
    exchange_matrix = summed / math.sqrt(rows_dev * n_grid)
    return (terms, exchange_matrix)


def solution(mesh):
    in_specs = (P("grid", "orb"), P(), P("grid", ("orb", "pts")), P(("orb", "pts"), "grid"))
    out_specs = (P(("orb", "pts"), "grid"), P(("orb", "pts"), "grid"))
    return jax.shard_map(
        per_device, mesh=mesh, in_specs=in_specs, out_specs=out_specs, check_vma=False
    )
```

profile of v0, /device:TPU:1, one launch (start us, length us, event | category | flops | bytes accessed | tf_op | source)
XLA Modules:
  0.0 432.0 jit_solution(11468976855244154880)
XLA Ops:
  7.2 0.8 compare_and_fusion.1
  8.0 0.8 fusion.17
  8.8 24.0 %gather_fusion = bf16[8192,128]{1,0:T(8,128)(2,1)S(1)} fusion(bf16[256,128]{1,0:T(8,128)(2,1)S(1)} %copy-done, s32[8192]{0:T(1024)S(1)} %fusion.17), kind=kCustom, calls=%fused_computation | custom fusion | bytes 4227072 | tf_op jit(solution)/shard_map/jit(_take)/gather | solution.py:58
  32.9 6.7 %select_convert_fusion = bf16[8192,128]{1,0:T(8,128)(2,1)} fusion(bf16[8192,128]{1,0:T(8,128)(2,1)S(1)} %gather_fusion, pred[8192]{0:T(1024)(128)(4,1)S(1)} %get-tuple-element.3, pred[8192]{0:T(1024)(128)(4,1)S(1)} %get-tuple-element.2), kind=kLoop, calls=%fused_computation.1 | loop fusion | flops 4194304 | bytes 4210688 | tf_op jit(solution)/shard_map/convert_element_type | solution.py:60
  39.7 82.1 %all-reduce.3.cloned.1.call-done = bf16[8192,128]{1,0:T(8,128)(2,1)} async-done(((bf16[8192,128]{1,0:T(8,128)(2,1)}), bf16[8192,128]{1,0:T(8,128)(2,1)}) %all-reduce.3.cloned.1.call-update) | async-done | bytes 2097168 | tf_op jit(solution)/shard_map/psum | solution.py:60
  121.8 1.3 constant_dynamic-slice_fusion.1
  123.1 1.0 constant_dynamic-slice_fusion
  124.1 1.2 pad_maximum_fusion
  125.3 0.7 all-gather.5.cloned.1.call-update
  126.0 147.0 %all-gather.3.cloned.1.call-done = bf16[5120,2048]{1,0:T(8,128)(2,1)} async-done(((bf16[5120,128]{1,0:T(8,128)(2,1)}), bf16[5120,2048]{1,0:T(8,128)(2,1)}) %all-gather.3.cloned.1.call-update) | async-done | bytes 20971536 | tf_op jit(solution)/shard_map/all_gather | solution.py:11
  273.0 14.2 %split.8 = bf16[4096,2048]{1,0:T(8,128)(2,1)} slice(bf16[5120,2048]{1,0:T(8,128)(2,1)} %all-gather.3.cloned.1.call-done), slice={[0:4096], [0:2048]} | slice | bytes 33554432 | tf_op jit(solution)/shard_map/split | solution.py:12
  287.2 6.2 %fusion = f32[256,2048]{1,0:T(8,128)S(1)} fusion(bf16[5120,2048]{1,0:T(8,128)(2,1)} %all-gather.3.cloned.1.call-done, bf16[256,1024]{1,0:T(8,128)(2,1)S(1)} %copy-done.2, bf16[4096,2048]{1,0:T(8,128)(2,1)} %split.8, s32[]{:T(128)S(6)} %select_n.28), kind=kOutput, calls=%fused_computation.2 | convolution fusion | flops 2148270080 | bytes 12058628 | tf_op jit(solution)/shard_map/dot_general | solution.py:72
  293.5 55.7 %all-reduce.4 = bf16[256,2048]{1,0:T(8,128)(2,1)S(1)} all-reduce(f32[256,2048]{1,0:T(8,128)S(1)} %fusion), channel_id=1, replica_groups=mesh['grid'=8,'orb'=16,'pts'=2] {'grid'}, use_global_device_ids=true, to_apply=%region_1.2 | all-reduce | flops 524288 | bytes 3145728 | tf_op jit(solution)/shard_map/psum | solution.py:73
  349.2 1.3 copy.7
  350.5 15.2 %all-to-all-start = ((bf16[256,32,64]{0,2,1:T(8,128)(2,1)}), bf16[256,32,64]{0,2,1:T(8,128)(2,1)S(1)}, u32[]{:S(2)}, u32[]{:S(2)}) async-start(bf16[256,32,64]{0,2,1:T(8,128)(2,1)} %bitcast.2), calls=%async_computation | async-start | bytes 2097152 | tf_op jit(solution)/shard_map/all_to_all | solution.py:74
  365.7 0.1 copy.9
  365.8 15.6 %all-to-all-done = bf16[256,32,64]{0,2,1:T(8,128)(2,1)S(1)} async-done(((bf16[256,32,64]{0,2,1:T(8,128)(2,1)}), bf16[256,32,64]{0,2,1:T(8,128)(2,1)S(1)}, u32[]{:S(2)}, u32[]{:S(2)}) %all-to-all-start) | async-done | bytes 1048608 | tf_op jit(solution)/shard_map/all_to_all | solution.py:74
  381.4 1.1 broadcast_in_dim.36
  382.5 6.0 %all-to-all-start.1 = ((bf16[16,256,128]{1,2,0:T(8,128)(2,1)}), bf16[16,256,128]{1,2,0:T(8,128)(2,1)S(1)}, u32[]{:S(2)}, u32[]{:S(2)}) async-start(bf16[16,256,128]{1,2,0:T(8,128)(2,1)} %broadcast_in_dim.36), calls=%async_computation.1 | async-start | bytes 2097152 | tf_op jit(solution)/shard_map/all_to_all | solution.py:23
  388.6 3.6 convolution_subtract_fusion
  392.2 13.4 %all-to-all-done.1 = bf16[16,256,128]{1,2,0:T(8,128)(2,1)S(1)} async-done(((bf16[16,256,128]{1,2,0:T(8,128)(2,1)}), bf16[16,256,128]{1,2,0:T(8,128)(2,1)S(1)}, u32[]{:S(2)}, u32[]{:S(2)}) %all-to-all-start.1) | async-done | bytes 1048608 | tf_op jit(solution)/shard_map/all_to_all | solution.py:23
  405.6 0.4 convolution_bitcast_fusion
  406.0 18.8 %all_to_all.29 = f32[8,64,256]{2,1,0:T(8,128)S(1)} all-to-all(f32[8,64,256]{2,1,0:T(8,128)S(1)} %convolution_bitcast_fusion), channel_id=1, replica_groups=mesh['grid'=8,'orb'=16,'pts'=2] {'grid'}, dimensions={0} | all-to-all | bytes 1048576 | tf_op jit(solution)/shard_map/all_to_all | solution.py:38
  424.9 0.6 broadcast_multiply_fusion
  (14 shorter events, 0.3 us)
Async XLA Ops:
  7.2 1.6 copy-start
  7.2 114.6 %all-reduce.3.cloned.1.call-start = ((), (), s32[]{:S(2)}) async-start(), calls=%async_computation.3 | async-start | bytes 4194304 | tf_op jit(solution)/shard_map/psum | solution.py:60
  39.6 233.4 %all-gather.3.cloned.1.call-start = ((), (), s32[]{:S(2)}) async-start(), calls=%async_computation.4 | async-start | bytes 22282240 | tf_op jit(solution)/shard_map/all_gather | solution.py:11
  125.3 263.3 %all-gather.5.cloned.1.call-start = ((), (), s32[]{:S(2)}) async-start(), calls=%async_computation.5 | async-start | bytes 4325376 | tf_op jit(solution)/shard_map/all_gather | solution.py:78
  126.0 161.3 %copy-start.2 = (bf16[256,1024]{1,0:T(8,128)(2,1)S(1)}, bf16[256,1024]{1,0:T(8,128)(2,1)}, u32[]{:S(2)}) copy-start(bf16[256,1024]{1,0:T(8,128)(2,1)} %param.7) | copy-start | bytes 1572868
  350.5 30.9 %all-to-all-start = ((bf16[256,32,64]{0,2,1:T(8,128)(2,1)}), bf16[256,32,64]{0,2,1:T(8,128)(2,1)S(1)}, u32[]{:S(2)}, u32[]{:S(2)}) async-start(bf16[256,32,64]{0,2,1:T(8,128)(2,1)} %bitcast.2), calls=%async_computation | async-start | bytes 2097152 | tf_op jit(solution)/shard_map/all_to_all | solution.py:74
  382.5 23.1 %all-to-all-start.1 = ((bf16[16,256,128]{1,2,0:T(8,128)(2,1)}), bf16[16,256,128]{1,2,0:T(8,128)(2,1)S(1)}, u32[]{:S(2)}, u32[]{:S(2)}) async-start(bf16[16,256,128]{1,2,0:T(8,128)(2,1)} %broadcast_in_dim.36), calls=%async_computation.1 | async-start | bytes 2097152 | tf_op jit(solution)/shard_map/all_to_all | solution.py:23
  392.2 33.3 %copy-start.1 = (f32[64,256]{1,0:T(8,128)}, f32[64,256]{1,0:T(8,128)S(1)}, u32[]{:S(2)}) copy-start(f32[64,256]{1,0:T(8,128)S(1)} %convolution_subtract_fusion) | copy-start | bytes 196612
Sparse Core Ops, SparseCore 0:
  39.7 82.0 all-reduce.2
  125.4 147.6 all-gather.2
  274.8 82.4 all-gather.4
where the time goes:
time: 433 us; the launch traced here: 432 us
  waiting for transfers between devices  259 us (60%)
  blocking collectives  74.5 us (17%)
  local copies, waits for them, and re-layouts  43.1 us (10%)
  starting transfers between devices  21.3 us (5%)
  between operations  13.9 us (3%)
  matrix products  10.2 us (2%)
  other arithmetic  10.1 us (2%)
    all_gather x1, waiting for transfers between devices, in_one_piece(): filled = lax.all_gather(both, axis, axis=dim, tiled=True)  147 us
    psum x1, waiting for transfers between devices, per_device(): picked = lax.psum(selected.astype(jnp.bfloat16), 'grid')  82.1 us
    psum x1, blocking collectives, per_device(): applied = lax.psum(partial_applied, 'grid').astype(jnp.bfloat16)  55.7 us
    gather x1, local copies, waits for them, and re-layouts, per_device(): taken = jnp.take(orbitals, clamped, axis=0).astype(jnp.float32)  24 us
    all_to_all x1, blocking collectives, sent_and_summed(): parts = lax.all_to_all(split_up(x, dim, peers), axis, 0, 0, tiled=True)  18.8 us
    all_to_all x1, waiting for transfers between devices, per_device(): lax.all_to_all(applied, ('orb', 'pts'), split_axis=1, concat_axis=0, tile...  15.6 us
    all_to_all x1, starting transfers between devices, per_device(): lax.all_to_all(applied, ('orb', 'pts'), split_axis=1, concat_axis=0, tile...  15.2 us
    split x1, local copies, waits for them, and re-layouts, in_one_piece(): jnp.split(filled, [sum(widths[:k]) for k in range(1, len(widths))], axis=...  14.2 us
  transfers between devices with their start and end apart: 5, of which 4 were waited for; matrix products, arithmetic and copies ran while one was open for 6% of the time, Pallas kernels for 0%

commit v1 on v0

--- a/solution.py
+++ b/solution.py
@@ -70,7 +70,7 @@
     )
     masked = (density * screened.astype(jnp.float32)).astype(jnp.bfloat16)
     partial_applied = jnp.dot(masked, point_full, preferred_element_type=jnp.float32)
-    applied = lax.psum(partial_applied, "grid").astype(jnp.bfloat16)
+    applied = jnp.sum(lax.all_gather(partial_applied, "grid"), axis=0).astype(jnp.bfloat16)
     columns = lax.all_to_all(applied, ("orb", "pts"), split_axis=1, concat_axis=0, tiled=True)
     initial = jnp.zeros((orbital_block, rows_dev), jnp.float32)
     terms = initial - lax.dot_general(

time: 433 us -> 602 us (1.39)
  waiting for transfers between devices: 259 us -> 478 us
  blocking collectives: 74.5 us -> 21.8 us
  other arithmetic: 10.1 us -> 17.9 us
    all_gather x0 -> x1, waiting for transfers between devices: none -> 169 us  [per_device(): lax.all_gather(partial_applied, 'grid')]
    all_gather x1, waiting for transfers between devices: 0.02 us -> 62.9 us  [per_device(): lax.all_gather(fitting, ('orb', 'pts'), axis=1, tiled=True)]
    psum x1 -> x0, blocking collectives: 55.7 us -> none  [per_device(): applied = lax.psum(partial_applied, 'grid').astype(jnp.bfloat16)]
    all_to_all x1, waiting for transfers between devices: 13.4 us -> 0.01 us  [sent_to_all(): return lax.all_to_all(copies, axis, split_axis=0, concat_axis=0, tiled=True)]
    reduce_sum x0 -> x1, other arithmetic: none -> 7.76 us  [per_device(): jnp.sum(lax.all_gather(partial_applied, 'grid'), axis=0)]
    all_to_all x1, starting transfers between devices: 15.2 us -> 7.7 us  [per_device(): lax.all_to_all(applied, ('orb', 'pts'), split_axis=1, concat_axis=0, tile...]
  transfers between devices with their start and end apart: 5 -> 6, of which waited for: 4 -> 5; matrix products, arithmetic and copies ran while one was open for 6% -> 2% of each run, Pallas kernels for 0% -> 0%
where the time goes in v1:
time: 602 us; the launch traced here: 601 us
  waiting for transfers between devices  478 us (79%)
  local copies, waits for them, and re-layouts  43.1 us (7%)
  blocking collectives  21.8 us (4%)
  other arithmetic  17.9 us (3%)
  starting transfers between devices  15.4 us (3%)
  between operations  13.9 us (2%)
  matrix products  11.5 us (2%)
    all_gather x1, waiting for transfers between devices, per_device(): lax.all_gather(partial_applied, 'grid')  169 us
    all_gather x1, waiting for transfers between devices, in_one_piece(): filled = lax.all_gather(both, axis, axis=dim, tiled=True)  148 us
    psum x1, waiting for transfers between devices, per_device(): picked = lax.psum(selected.astype(jnp.bfloat16), 'grid')  82.1 us
    all_gather x1, waiting for transfers between devices, per_device(): lax.all_gather(fitting, ('orb', 'pts'), axis=1, tiled=True)  62.9 us
    gather x1, local copies, waits for them, and re-layouts, per_device(): taken = jnp.take(orbitals, clamped, axis=0).astype(jnp.float32)  24 us
    all_to_all x1, blocking collectives, sent_and_summed(): parts = lax.all_to_all(split_up(x, dim, peers), axis, 0, 0, tiled=True)  21.8 us
    all_to_all x1, waiting for transfers between devices, per_device(): lax.all_to_all(applied, ('orb', 'pts'), split_axis=1, concat_axis=0, tile...  15.5 us
    split x1, local copies, waits for them, and re-layouts, in_one_piece(): jnp.split(filled, [sum(widths[:k]) for k in range(1, len(widths))], axis=...  14.2 us
  transfers between devices with their start and end apart: 6, of which 5 were waited for; matrix products, arithmetic and copies ran while one was open for 2% of the time, Pallas kernels for 0%

profile of v1, /device:TPU:1, one launch (start us, length us, event | category | flops | bytes accessed | tf_op | source)
XLA Modules:
  0.0 601.4 jit_solution(1006111958226428812)
XLA Ops:
  7.2 0.8 compare_and_fusion.1
  8.0 0.8 fusion.17
  8.8 24.0 %gather_fusion = bf16[8192,128]{1,0:T(8,128)(2,1)S(1)} fusion(bf16[256,128]{1,0:T(8,128)(2,1)S(1)} %copy-done, s32[8192]{0:T(1024)S(1)} %fusion.17), kind=kCustom, calls=%fused_computation | custom fusion | bytes 4227072 | tf_op jit(solution)/shard_map/jit(_take)/gather | solution.py:58
  32.9 6.7 %select_convert_fusion = bf16[8192,128]{1,0:T(8,128)(2,1)} fusion(bf16[8192,128]{1,0:T(8,128)(2,1)S(1)} %gather_fusion, pred[8192]{0:T(1024)(128)(4,1)S(1)} %get-tuple-element.3, pred[8192]{0:T(1024)(128)(4,1)S(1)} %get-tuple-element.2), kind=kLoop, calls=%fused_computation.1 | loop fusion | flops 4194304 | bytes 4210688 | tf_op jit(solution)/shard_map/convert_element_type | solution.py:60
  39.7 82.1 %all-reduce.2.cloned.1.call-done = bf16[8192,128]{1,0:T(8,128)(2,1)} async-done(((bf16[8192,128]{1,0:T(8,128)(2,1)}), bf16[8192,128]{1,0:T(8,128)(2,1)}) %all-reduce.2.cloned.1.call-update) | async-done | bytes 2097168 | tf_op jit(solution)/shard_map/psum | solution.py:60
  121.8 1.3 constant_dynamic-slice_fusion.1
  123.1 1.0 constant_dynamic-slice_fusion
  124.1 1.2 pad_maximum_fusion
  125.3 147.7 %all-gather.5.cloned.1.call-done = bf16[5120,2048]{1,0:T(8,128)(2,1)} async-done(((bf16[5120,128]{1,0:T(8,128)(2,1)}), bf16[5120,2048]{1,0:T(8,128)(2,1)}) %all-gather.5.cloned.1.call-update) | async-done | bytes 20971536 | tf_op jit(solution)/shard_map/all_gather | solution.py:11
  273.0 14.2 %split.8 = bf16[4096,2048]{1,0:T(8,128)(2,1)} slice(bf16[5120,2048]{1,0:T(8,128)(2,1)} %all-gather.5.cloned.1.call-done), slice={[0:4096], [0:2048]} | slice | bytes 33554432 | tf_op jit(solution)/shard_map/split | solution.py:12
  287.2 7.4 %fusion = f32[256,2048]{1,0:T(8,128)} fusion(bf16[5120,2048]{1,0:T(8,128)(2,1)} %all-gather.5.cloned.1.call-done, bf16[256,1024]{1,0:T(8,128)(2,1)S(1)} %copy-done.2, bf16[4096,2048]{1,0:T(8,128)(2,1)} %split.8, s32[]{:T(128)S(6)} %select_n.28), kind=kOutput, calls=%fused_computation.2 | convolution fusion | flops 2148270080 | bytes 12058628 | tf_op jit(solution)/shard_map/dot_general | solution.py:72
  294.7 0.5 all-gather.7.cloned.1.call-update
  295.3 169.0 %all-gather.9.cloned.1.call-done = f32[2048,2048]{1,0:T(8,128)} async-done(((f32[256,2048]{1,0:T(8,128)}), f32[2048,2048]{1,0:T(8,128)}) %all-gather.9.cloned.1.call-update) | async-done | bytes 16777232 | tf_op jit(solution)/shard_map/all_gather | solution.py:73
  464.3 7.8 %reduce_sum.18 = bf16[256,2048]{1,0:T(8,128)(2,1)S(1)} reduce(f32[8,256,2048]{2,1,0:T(8,128)} %bitcast.22, f32[]{:T(128)} %constant.14.clone.1), dimensions={0}, to_apply=%region_1.2 | reduce | flops 3670016 | bytes 17825796 | tf_op jit(solution)/shard_map/reduce_sum | solution.py:73
  472.1 1.3 copy.9
  473.4 7.7 %all-to-all-start = ((bf16[256,32,64]{0,2,1:T(8,128)(2,1)}), bf16[256,32,64]{0,2,1:T(8,128)(2,1)S(1)}, u32[]{:S(2)}, u32[]{:S(2)}) async-start(bf16[256,32,64]{0,2,1:T(8,128)(2,1)} %bitcast.3), calls=%async_computation | async-start | bytes 2097152 | tf_op jit(solution)/shard_map/all_to_all | solution.py:74
  481.2 15.5 %all-to-all-done = bf16[256,32,64]{0,2,1:T(8,128)(2,1)S(1)} async-done(((bf16[256,32,64]{0,2,1:T(8,128)(2,1)}), bf16[256,32,64]{0,2,1:T(8,128)(2,1)S(1)}, u32[]{:S(2)}, u32[]{:S(2)}) %all-to-all-start) | async-done | bytes 1048608 | tf_op jit(solution)/shard_map/all_to_all | solution.py:74
  496.7 1.1 broadcast_in_dim.36
  497.7 7.6 %all-to-all-start.1 = ((bf16[16,256,128]{1,2,0:T(8,128)(2,1)}), bf16[16,256,128]{1,2,0:T(8,128)(2,1)S(1)}, u32[]{:S(2)}, u32[]{:S(2)}) async-start(bf16[16,256,128]{1,2,0:T(8,128)(2,1)} %broadcast_in_dim.36), calls=%async_computation.1 | async-start | bytes 2097152 | tf_op jit(solution)/shard_map/all_to_all | solution.py:23
  505.4 62.9 %all-gather.7.cloned.1.call-done = bf16[256,8192]{1,0:T(8,128)(2,1)} async-done(((bf16[256,256]{1,0:T(8,128)(2,1)}), bf16[256,8192]{1,0:T(8,128)(2,1)}) %all-gather.7.cloned.1.call-update) | async-done | bytes 4194320 | tf_op jit(solution)/shard_map/all_gather | solution.py:78
  568.3 3.6 convolution_subtract_fusion
  571.9 0.4 convolution_bitcast_fusion
  572.3 21.8 %all_to_all.26 = f32[8,64,256]{2,1,0:T(8,128)S(1)} all-to-all(f32[8,64,256]{2,1,0:T(8,128)S(1)} %convolution_bitcast_fusion), channel_id=1, replica_groups=mesh['grid'=8,'orb'=16,'pts'=2] {'grid'}, dimensions={0} | all-to-all | bytes 1048576 | tf_op jit(solution)/shard_map/all_to_all | solution.py:38
  594.2 0.6 broadcast_multiply_fusion
  (17 shorter events, 0.4 us)
Async XLA Ops:
  7.2 1.6 copy-start
  7.2 114.6 %all-reduce.2.cloned.1.call-start = ((), (), s32[]{:S(2)}) async-start(), calls=%async_computation.3 | async-start | bytes 4194304 | tf_op jit(solution)/shard_map/psum | solution.py:60
  39.6 233.4 %all-gather.5.cloned.1.call-start = ((), (), s32[]{:S(2)}) async-start(), calls=%async_computation.4 | async-start | bytes 22282240 | tf_op jit(solution)/shard_map/all_gather | solution.py:11
  125.2 339.0 %all-gather.9.cloned.1.call-start = ((), (), s32[]{:S(2)}) async-start(), calls=%async_computation.6 | async-start | bytes 18874368 | tf_op jit(solution)/shard_map/all_gather | solution.py:73
  125.3 161.9 %copy-start.2 = (bf16[256,1024]{1,0:T(8,128)(2,1)S(1)}, bf16[256,1024]{1,0:T(8,128)(2,1)}, u32[]{:S(2)}) copy-start(bf16[256,1024]{1,0:T(8,128)(2,1)} %param.7) | copy-start | bytes 1572868
  294.7 273.6 %all-gather.7.cloned.1.call-start = ((), (), s32[]{:S(2)}) async-start(), calls=%async_computation.5 | async-start | bytes 4325376 | tf_op jit(solution)/shard_map/all_gather | solution.py:78
  473.4 23.3 %all-to-all-start = ((bf16[256,32,64]{0,2,1:T(8,128)(2,1)}), bf16[256,32,64]{0,2,1:T(8,128)(2,1)S(1)}, u32[]{:S(2)}, u32[]{:S(2)}) async-start(bf16[256,32,64]{0,2,1:T(8,128)(2,1)} %bitcast.3), calls=%async_computation | async-start | bytes 2097152 | tf_op jit(solution)/shard_map/all_to_all | solution.py:74
  497.7 74.1 %all-to-all-start.1 = ((bf16[16,256,128]{1,2,0:T(8,128)(2,1)}), bf16[16,256,128]{1,2,0:T(8,128)(2,1)S(1)}, u32[]{:S(2)}, u32[]{:S(2)}) async-start(bf16[16,256,128]{1,2,0:T(8,128)(2,1)} %broadcast_in_dim.36), calls=%async_computation.1 | async-start | bytes 2097152 | tf_op jit(solution)/shard_map/all_to_all | solution.py:23
  571.9 23.0 %copy-start.1 = (f32[64,256]{1,0:T(8,128)}, f32[64,256]{1,0:T(8,128)S(1)}, u32[]{:S(2)}) copy-start(f32[64,256]{1,0:T(8,128)S(1)} %convolution_subtract_fusion) | copy-start | bytes 196612
Sparse Core Ops, SparseCore 0:
  39.7 82.0 all-reduce.1
  125.4 147.6 all-gather.4
  294.8 169.4 all-gather.8
  465.9 102.3 all-gather.6
